TPU v7x, 32 devices: a whole 2x2x4 slice. The times are simulated.
32 devices in a mesh: grid: 8 (over z, x), band: 4 (over y, core).
Axes of the slice: x: 2, y: 2, z: 4, core: 2. Of those that a mesh axis runs over, the one named last changes fastest.
Arguments:
- psi: bfloat16 [2048, 16, 512], P('band', 'grid'), may hold values from -6 to 6
- ritz_matrix: float32 [2048, 2048], P('band'), may hold values from -0.125 to 0.125
- potential: float32 [16, 512], P('grid'), may hold values from 0.5 to 10, as said below
Outputs:
- rotated: bfloat16 [2048, 16, 512], P('band', 'grid')
- search: bfloat16 [2048, 16, 512], P('band', 'grid')
Inputs may be any that keep to these rules, and one draw needn't show every extreme that they name: `potential`: positive everywhere.
All inputs are finite; a program needn't handle non-finite values.
Results may differ from a plain program's by a relative error of at most 0.0049.
Values may be sent and summed in bfloat16 or wider, within the bound.
A program may use at most 64 MiB of HBM per device.

v0:
```python
import jax
import jax.numpy as jnp
from jax import lax
from jax.sharding import PartitionSpec as P

NZ = 64
epsilon_mean = 1e-06


def with_halo(value, sides, width):
    for axis, dim in sides:
        count, length = (lax.axis_size(axis), value.shape[dim])
        up = [(i, (i + 1) % count) for i in range(count)]
        down = [(j, i) for i, j in up]
        last = lax.slice_in_dim(value, length - width, length, axis=dim)
        first = lax.slice_in_dim(value, 0, width, axis=dim)
        before = lax.ppermute(last, axis, up)
        after = lax.ppermute(first, axis, down)
        value = jnp.concatenate([before, value, after], axis=dim)
    return value


def apply_residual(padded, potential):
    center = padded[:, 1:-1].astype(jnp.float32)
    neighbours = padded[:, 2:].astype(jnp.float32) + padded[:, :-2].astype(jnp.float32)
    shaped = center.reshape(center.shape[0], center.shape[1], -1, NZ)
    across = (
        jnp.roll(shaped, 1, 2)
        + jnp.roll(shaped, -1, 2)
        + jnp.roll(shaped, 1, 3)
        + jnp.roll(shaped, -1, 3)
    )
    laplacian = neighbours + across.reshape(center.shape) - 6.0 * center
    resid = -0.5 * laplacian + potential[None] * center
    return (center, resid)


def shards(psi, ritz_matrix, potential):
    band_count = psi.shape[0]
    planes_dev = psi.shape[1]
    face_cells = psi.shape[2]
    piece = lax.all_gather(psi, "band", axis=0, tiled=True)
    flattened = piece.reshape(piece.shape[0], -1).astype(jnp.float32)
    folded = jnp.dot(ritz_matrix, flattened, precision=lax.Precision.HIGHEST)
    rotated = folded.reshape(band_count, planes_dev, face_cells).astype(jnp.bfloat16)
    padded = with_halo(rotated, (("grid", 1),), 1)
    center, resid = apply_residual(padded, potential)
    total_cells = planes_dev * face_cells * lax.axis_size("grid")
    cross_local = jnp.sum(center * resid, axis=(1, 2))
    self_local = jnp.sum(center * center, axis=(1, 2))
    resid_local = jnp.sum(resid * resid, axis=(1, 2))
    cross_sum, self_sum, resid_sum = lax.psum((cross_local, self_local, resid_local), "grid")
    m_cross = cross_sum / total_cells
    m_plain = self_sum / total_cells
    ratio = m_cross / (m_plain + epsilon_mean)
    direction = resid - ratio[:, None, None] * center
    m_dir = resid_sum / total_cells - 2.0 * ratio * m_cross + ratio * ratio * m_plain
    search = direction * lax.rsqrt(m_dir + epsilon_mean)[:, None, None]
    return (rotated, search.astype(jnp.bfloat16))


def solution(mesh):
    return jax.shard_map(
        shards,
        mesh=mesh,
        in_specs=(P("band", "grid", None), P("band", None), P("grid", None)),
        out_specs=(P("band", "grid", None), P("band", "grid", None)),
        check_vma=False,
    )
```

profile of v0, /device:TPU:0, one launch (start us, length us, event | category | flops | bytes accessed | tf_op | source)
XLA Modules:
  0.0 136.8 jit_solution(16779906986271277849)
XLA Ops:
  7.2 0.0 all-gather.2.cloned.1.call-start
  7.2 0.7 all-gather.2.cloned.1.call-update
  7.9 38.8 %all-gather.2.cloned.1.call-done = bf16[2048,2,512]{2,1,0:T(2,128)(2,1)} async-done(((bf16[512,2,512]{2,1,0:T(2,128)(2,1)}), bf16[2048,2,512]{2,1,0:T(2,128)(2,1)}) %all-gather.2.cloned.1.call-update) | async-done | bytes 4194320 | tf_op jit(solution)/shard_map/all_gather | solution.py:42
  46.7 11.2 %copy.11 = bf16[2048,2,512]{0,2,1:T(8,128)(2,1)} copy(bf16[2048,2,512]{2,1,0:T(2,128)(2,1)} %all-gather.2.cloned.1.call-done) | data formatting | bytes 8388608 | tf_op jit(solution)/shard_map/reshape | solution.py:43
  58.0 9.8 %fusion.13 = bf16[512,2,512]{0,2,1:T(8,128)(2,1)S(1)} fusion(bf16[2048,2,512]{0,2,1:T(8,128)(2,1)} %copy.11, f32[512,2048]{1,0:T(8,128)} %param.4), kind=kOutput, calls=%fused_computation.21 | convolution fusion | flops 12885426176 | bytes 9437184 | tf_op jit(solution)/shard_map/dot_general | solution.py:44
  67.8 2.5 %fusion.19 = (f32[512,2,8,63]{0,3,2,1:T(8,128)}, f32[512,2,8,63]{0,3,2,1:T(8,128)}) fusion(bf16[512,2,8,64]{0,3,2,1:T(8,128)(2,1)S(1)} %bitcast.26), kind=kLoop, calls=%fused_computation.27 | loop fusion | bytes 8257536 | tf_op jit(solution)/shard_map/jit(_roll_static)/slice | solution.py:31
  70.3 0.8 fusion.22
  71.2 1.0 fusion.18
  72.2 2.1 %copy.9 = bf16[512,2,512]{2,1,0:T(2,128)(2,1)} copy(bf16[512,2,512]{0,2,1:T(8,128)(2,1)S(1)} %fusion.13) | data formatting | bytes 2097152
  74.3 4.2 %collective-permute-start = (bf16[512,1,512]{0,2,1:T(8,128)(2,1)}, bf16[512,1,512]{0,2,1:T(8,128)(2,1)S(1)}, u32[]{:S(2)}, u32[]{:S(2)}) collective-permute-start(bf16[512,1,512]{0,2,1:T(8,128)(2,1)} %get-tuple-element.12), channel_id=1, source_target_pairs={{4,0},{8,4},{12,8},{16,12},{20,16},{24,20},{28,24},{0,28},{5,1},{9... | collective-permute-start | bytes 1572872 | tf_op jit(solution)/shard_map/ppermute | solution.py:18
  78.5 0.0 copy-start
  78.5 0.0 copy-start.1
  78.5 0.0 copy-start.4
  78.5 0.0 collective-permute-start.1
  78.5 0.5 fusion.21
  79.0 1.1 copy-done
  80.1 0.6 copy-done.1
  80.7 0.0 copy-done.4
  80.7 0.0 copy-start.5
  80.7 1.1 fusion.12
  81.8 18.0 %collective-permute-done = bf16[512,1,512]{0,2,1:T(8,128)(2,1)S(1)} collective-permute-done((bf16[512,1,512]{0,2,1:T(8,128)(2,1)}, bf16[512,1,512]{0,2,1:T(8,128)(2,1)S(1)}, u32[]{:S(2)}, u32[]{:S(2)}) %collective-permute-start) | collective-permute-done | bytes 524320 | tf_op jit(solution)/shard_map/ppermute | solution.py:18
  99.8 0.0 copy-start.2
  99.8 0.0 collective-permute-done.1
  99.8 0.0 copy-done.5
  99.8 0.0 copy-start.3
  99.8 1.3 fusion.6
  101.1 0.0 copy-done.2
  101.2 0.0 copy-done.3
  101.2 21.9 %all-reduce = (f32[512]{0:T(512)S(1)}, f32[512]{0:T(512)S(1)}, f32[512]{0:T(512)S(1)}) all-reduce(f32[512]{0:T(512)S(1)} %get-tuple-element.7, f32[512]{0:T(512)S(1)} %get-tuple-element.8, f32[512]{0:T(512)S(1)} %get-tuple-element.6), channel_id=1, replica_groups=mesh['grid'=8,'band'=4] {'grid'}, use_global_device_ids=true, to_apply=%region_5.6 | all-reduce | flops 1536 | bytes 12288 | tf_op jit(solution)/shard_map/psum | solution.py:52
  123.1 3.2 %fusion.10 = bf16[512,2,512]{0,2,1:T(8,128)(2,1)} fusion(bf16[512,2,512]{0,2,1:T(8,128)(2,1)S(1)} %fusion.13, f32[512]{0:T(512)S(1)} %get-tuple-element.23, f32[512]{0:T(512)S(1)} %get-tuple-element.22, f32[2,512]{1,0:T(2,128)S(1)} %copy-done.5, f32[512,2,8,64]{0,3,2,1:T(8,128)S(1)} %fusion.12, bf16[512,1,512]{0,2,1:T(8,128)(2,1)} %copy-done.3, ...), kind=kLoop, calls=%fused_computation.15 | loop fusion | flops 8388608 | bytes 5251072 | tf_op jit(solution)/shard_map/convert_element_type | solution.py:59
  126.3 3.7 %copy.10 = bf16[512,2,512]{2,1,0:T(2,128)(2,1)} copy(bf16[512,2,512]{0,2,1:T(8,128)(2,1)} %fusion.10) | data formatting | bytes 2097152
  (2 shorter events, 0.1 us)
Async XLA Ops:
  7.2 39.6 %all-gather.2.cloned.1.call-start = ((), (), s32[]{:S(2)}) async-start(), calls=%async_computation | async-start | bytes 5242880 | tf_op jit(solution)/shard_map/all_gather | solution.py:42
  74.3 25.5 %collective-permute-start = (bf16[512,1,512]{0,2,1:T(8,128)(2,1)}, bf16[512,1,512]{0,2,1:T(8,128)(2,1)S(1)}, u32[]{:S(2)}, u32[]{:S(2)}) collective-permute-start(bf16[512,1,512]{0,2,1:T(8,128)(2,1)} %get-tuple-element.12), channel_id=1, source_target_pairs={{4,0},{8,4},{12,8},{16,12},{20,16},{24,20},{28,24},{0,28},{5,1},{9... | collective-permute-start | bytes 1572872 | tf_op jit(solution)/shard_map/ppermute | solution.py:18
  78.5 1.6 %copy-start = (f32[512,2,8,63]{0,3,2,1:T(8,128)S(1)}, f32[512,2,8,63]{0,3,2,1:T(8,128)}, u32[]{:S(2)}) copy-start(f32[512,2,8,63]{0,3,2,1:T(8,128)} %get-tuple-element.14) | copy-start | bytes 6193156
  78.5 2.2 %copy-start.1 = (f32[512,2,8,63]{0,3,2,1:T(8,128)S(1)}, f32[512,2,8,63]{0,3,2,1:T(8,128)}, u32[]{:S(2)}) copy-start(f32[512,2,8,63]{0,3,2,1:T(8,128)} %get-tuple-element.15) | copy-start | bytes 6193156
  78.5 2.2 %copy-start.4 = (f32[512,2,1,64]{0,3,2,1:T(8,128)S(1)}, f32[512,2,1,64]{0,3,2,1:T(8,128)}, u32[]{:S(2)}) copy-start(f32[512,2,1,64]{0,3,2,1:T(8,128)} %get-tuple-element.21) | copy-start | bytes 786436
  78.5 21.3 %collective-permute-start.1 = (bf16[512,1,512]{0,2,1:T(8,128)(2,1)}, bf16[512,1,512]{0,2,1:T(8,128)(2,1)S(1)}, u32[]{:S(2)}, u32[]{:S(2)}) collective-permute-start(bf16[512,1,512]{0,2,1:T(8,128)(2,1)} %get-tuple-element.13), channel_id=1, source_target_pairs={{0,4},{4,8},{8,12},{12,16},{16,20},{20,24},{24,28},{28,0},{1,5},{5... | collective-permute-start | bytes 1572872 | tf_op jit(solution)/shard_map/ppermute | solution.py:17
  80.7 19.1 %copy-start.5 = (f32[2,512]{1,0:T(2,128)S(1)}, f32[2,512]{1,0:T(2,128)}, u32[]{:S(2)}) copy-start(f32[2,512]{1,0:T(2,128)} %param.5) | copy-start | bytes 12292
  99.8 1.4 copy-start.2
  99.8 1.4 copy-start.3
Sparse Core Ops, SparseCore 0:
  9.5 37.1 all-gather.1
where the time goes:
time: 137 us
  waiting for transfers between devices  57.5 us (42%)
  local copies, waits for them, and re-layouts  23.6 us (17%)
  blocking collectives  21.9 us (16%)
  between operations  14.1 us (10%)
  matrix products  9.83 us (7%)
  other arithmetic  5.62 us (4%)
  starting transfers between devices  4.28 us (3%)
    all_gather x1, waiting for transfers between devices, shards(): piece = lax.all_gather(psi, 'band', axis=0, tiled=True)  38.8 us
    psum x1, blocking collectives, shards(): lax.psum((cross_local, self_local, resid_local), 'grid')  21.9 us
    ppermute x1, waiting for transfers between devices, with_halo(): after = lax.ppermute(first, axis, down)  18 us
    reshape x1, local copies, waits for them, and re-layouts, shards(): flattened = piece.reshape(piece.shape[0], -1).astype(jnp.float32)  11.2 us
    dot_general x1, matrix products, shards(): folded = jnp.dot(ritz_matrix, flattened, precision=lax.Precision.HIGHEST)  9.83 us
    unnamed x14, local copies, waits for them, and re-layouts  7.49 us
    ppermute x1, starting transfers between devices, with_halo(): after = lax.ppermute(first, axis, down)  4.24 us
    convert_element_type x1, other arithmetic, shards(): return (rotated, search.astype(jnp.bfloat16))  3.19 us
  transfers between devices with their start and end apart: 3, of which 2 were waited for; matrix products, arithmetic and copies ran while one was open for 1% of the time, Pallas kernels for 0%

commit v1 on v0

--- a/solution.py
+++ b/solution.py
@@ -39,7 +39,12 @@
     band_count = psi.shape[0]
     planes_dev = psi.shape[1]
     face_cells = psi.shape[2]
-    piece = lax.all_gather(psi, "band", axis=0, tiled=True)
+    ring = [psi]
+    for hop in range(3):
+        ring.append(lax.ppermute(ring[-1], "band", [(dev, (dev + 1) % 4) for dev in range(4)]))
+    piece = jnp.roll(
+        jnp.concatenate(ring[::-1], axis=0), (lax.axis_index("band") + 1) * ring[0].shape[0], axis=0
+    )
     flattened = piece.reshape(piece.shape[0], -1).astype(jnp.float32)
     folded = jnp.dot(ritz_matrix, flattened, precision=lax.Precision.HIGHEST)
     rotated = folded.reshape(band_count, planes_dev, face_cells).astype(jnp.bfloat16)

time: 137 us -> 122 us (0.89)
  between operations: 14.1 us -> 0.75 us
  waiting for transfers between devices: 57.5 us -> 62.3 us
  local copies, waits for them, and re-layouts: 23.6 us -> 20.6 us
  other arithmetic: 5.62 us -> 3.73 us
  matrix products: 9.83 us -> 8.04 us
  starting transfers between devices: 4.28 us -> 6.03 us
    ppermute x0 -> x3, waiting for transfers between devices: none -> 43 us  [shards(): lax.ppermute(ring[-1], 'band', [(dev, (dev + 1) % 4) for dev in range(4)])]
    all_gather x1 -> x0, waiting for transfers between devices: 38.8 us -> none  [shards(): piece = lax.all_gather(psi, 'band', axis=0, tiled=True)]
    ppermute x1, waiting for transfers between devices: 0.01 us -> 17 us  [with_halo(): before = lax.ppermute(last, axis, up)]
    ppermute x1, waiting for transfers between devices: 18 us -> 2.21 us  [with_halo(): after = lax.ppermute(first, axis, down)]
    reshape x1 -> x0, local copies, waits for them, and re-layouts: 11.2 us -> none  [shards(): flattened = piece.reshape(piece.shape[0], -1).astype(jnp.float32)]
    unnamed x14 -> x20, local copies, waits for them, and re-layouts: 7.49 us -> 13.4 us
    dynamic_slice x0 -> x1, local copies, waits for them, and re-layouts: none -> 3.19 us  [shards(): jnp.roll(jnp.concatenate(ring[::-1], axis=0), (lax.axis_index('band') + 1...]
    ppermute x1, starting transfers between devices: 0.01 us -> 2.32 us  [with_halo(): before = lax.ppermute(last, axis, up)]
  transfers between devices with their start and end apart: 3 -> 5, of which waited for: 2 -> 5; matrix products, arithmetic and copies ran while one was open for 1% -> 1% of each run, Pallas kernels for 0% -> 0%
where the time goes in v1:
time: 122 us
  waiting for transfers between devices  62.3 us (51%)
  blocking collectives  20.7 us (17%)
  local copies, waits for them, and re-layouts  20.6 us (17%)
  matrix products  8.04 us (7%)
  starting transfers between devices  6.03 us (5%)
  other arithmetic  3.73 us (3%)
    ppermute x3, waiting for transfers between devices, shards(): lax.ppermute(ring[-1], 'band', [(dev, (dev + 1) % 4) for dev in range(4)])  43 us
    psum x1, blocking collectives, shards(): lax.psum((cross_local, self_local, resid_local), 'grid')  20.7 us
    ppermute x1, waiting for transfers between devices, with_halo(): before = lax.ppermute(last, axis, up)  17 us
    unnamed x20, local copies, waits for them, and re-layouts  13.4 us
    dot_general x1, matrix products, shards(): folded = jnp.dot(ritz_matrix, flattened, precision=lax.Precision.HIGHEST)  8.04 us
    dynamic_slice x1, local copies, waits for them, and re-layouts, shards(): jnp.roll(jnp.concatenate(ring[::-1], axis=0), (lax.axis_index('band') + 1...  3.19 us
    ppermute x1, starting transfers between devices, with_halo(): after = lax.ppermute(first, axis, down)  3.12 us
  transfers between devices with their start and end apart: 5, of which 5 were waited for; matrix products, arithmetic and copies ran while one was open for 1% of the time, Pallas kernels for 0%

profile of v1, /device:TPU:0, one launch (start us, length us, event | category | flops | bytes accessed | tf_op | source)
XLA Modules:
  0.0 122.1 jit_solution(5828988405431060337)
XLA Ops:
  0.6 0.5 collective-permute-start
  1.2 14.6 %collective-permute-done = bf16[512,2,512]{2,1,0:T(2,128)(2,1)S(1)} collective-permute-done((bf16[512,2,512]{2,1,0:T(2,128)(2,1)}, bf16[512,2,512]{2,1,0:T(2,128)(2,1)S(1)}, u32[]{:S(2)}, u32[]{:S(2)}) %collective-permute-start) | collective-permute-done | bytes 1048608 | tf_op jit(solution)/shard_map/ppermute | solution.py:44
  15.8 0.0 collective-permute-start.1
  15.9 14.2 %collective-permute-done.1 = bf16[512,2,512]{2,1,0:T(2,128)(2,1)S(1)} collective-permute-done((bf16[512,2,512]{2,1,0:T(2,128)(2,1)S(1)}, bf16[512,2,512]{2,1,0:T(2,128)(2,1)S(1)}, u32[]{:S(2)}, u32[]{:S(2)}) %collective-permute-start.1) | collective-permute-done | bytes 1048608 | tf_op jit(solution)/shard_map/ppermute | solution.py:44
  30.0 0.0 collective-permute-start.2
  30.0 14.2 %collective-permute-done.2 = bf16[512,2,512]{2,1,0:T(2,128)(2,1)S(1)} collective-permute-done((bf16[512,2,512]{2,1,0:T(2,128)(2,1)S(1)}, bf16[512,2,512]{2,1,0:T(2,128)(2,1)S(1)}, u32[]{:S(2)}, u32[]{:S(2)}) %collective-permute-start.2) | collective-permute-done | bytes 1048608 | tf_op jit(solution)/shard_map/ppermute | solution.py:44
  44.3 0.7 constant_dynamic-update-slice_fusion.7
  45.0 0.0 copy-start.1
  45.0 0.8 constant_dynamic-update-slice_fusion.6
  45.8 0.8 constant_dynamic-update-slice_fusion.5
  46.6 0.0 copy-done.1
  46.6 0.8 constant_dynamic-update-slice_fusion.4
  47.4 0.8 constant_dynamic-update-slice_fusion.3
  48.2 0.8 constant_dynamic-update-slice_fusion.2
  49.0 0.8 constant_dynamic-update-slice_fusion.1
  49.7 0.8 constant_dynamic-update-slice_fusion
  50.5 3.2 %constant_dynamic-slice_fusion = bf16[2048,2,512]{2,1,0:T(2,128)(2,1)S(1)} fusion(bf16[4096,2,512]{2,1,0:T(2,128)(2,1)S(1)} %constant_dynamic-update-slice_fusion, s32[]{:T(128)S(6)} %select_n.14), kind=kLoop, calls=%fused_computation.30 | loop fusion | bytes 8388612 | tf_op jit(solution)/shard_map/jit(_roll_dynamic)/dynamic_slice | solution.py:45
  53.7 0.0 copy-start.4
  53.7 1.2 copy.14
  54.9 1.0 copy-done.4
  55.9 8.0 %multiply_reduce_fusion.1 = (f32[512]{0:T(512)S(1)}, bf16[1024,512]{1,0:T(8,128)(2,1)S(1)}) fusion(bf16[2048,1024]{1,0:T(8,128)(2,1)S(1)} %bitcast.25, f32[512,2048]{1,0:T(8,128)S(1)} %copy-done.4), kind=kOutput, calls=%fused_computation.16 | convolution fusion | flops 12886999040 | bytes 9439232 | tf_op jit(solution)/shard_map/dot_general | solution.py:49
  64.0 0.8 fusion.14
  64.7 1.9 %fusion.11 = (f32[512,2,8,63]{0,3,2,1:T(8,128)S(1)}, f32[512,2,8,63]{0,3,2,1:T(8,128)}) fusion(bf16[512,2,8,64]{0,3,2,1:T(8,128)(2,1)S(1)} %bitcast.18), kind=kLoop, calls=%fused_computation.32 | loop fusion | bytes 8257536 | tf_op jit(solution)/shard_map/jit(_roll_static)/slice | solution.py:31
  66.7 2.1 %copy.12 = bf16[512,2,512]{2,1,0:T(2,128)(2,1)} copy(bf16[512,2,512]{0,2,1:T(8,128)(2,1)S(1)} %bitcast.20) | data formatting | bytes 2097152
  68.8 0.1 fusion.10
  68.8 2.3 %collective-permute-start.4 = (bf16[512,1,512]{0,2,1:T(8,128)(2,1)S(1)}, bf16[512,1,512]{0,2,1:T(8,128)(2,1)S(1)}, u32[]{:S(2)}, u32[]{:S(2)}) collective-permute-start(bf16[512,1,512]{0,2,1:T(8,128)(2,1)S(1)} %get-tuple-element.13), channel_id=1, source_target_pairs={{0,4},{4,8},{8,12},{12,16},{16,20},{20,24},{24,28},{28,0},{1,5},{5... | collective-permute-start | bytes 1572872 | tf_op jit(solution)/shard_map/ppermute | solution.py:17
  71.2 0.0 copy-start
  71.2 0.0 copy-start.2
  71.2 3.1 %collective-permute-start.3 = (bf16[512,1,512]{0,2,1:T(8,128)(2,1)S(1)}, bf16[512,1,512]{0,2,1:T(8,128)(2,1)S(1)}, u32[]{:S(2)}, u32[]{:S(2)}) collective-permute-start(bf16[512,1,512]{0,2,1:T(8,128)(2,1)S(1)} %get-tuple-element.12), channel_id=1, source_target_pairs={{4,0},{8,4},{12,8},{16,12},{20,16},{24,20},{28,24},{0,28},{5,1},{9... | collective-permute-start | bytes 1572872 | tf_op jit(solution)/shard_map/ppermute | solution.py:18
  74.3 0.5 fusion.13
  74.8 0.0 copy-done
  74.8 0.0 copy-done.2
  74.8 0.0 copy-start.3
  74.8 1.1 fusion.8
  75.9 17.0 %collective-permute-done.4 = bf16[512,1,512]{0,2,1:T(8,128)(2,1)S(1)} collective-permute-done((bf16[512,1,512]{0,2,1:T(8,128)(2,1)S(1)}, bf16[512,1,512]{0,2,1:T(8,128)(2,1)S(1)}, u32[]{:S(2)}, u32[]{:S(2)}) %collective-permute-start.4) | collective-permute-done | bytes 524320 | tf_op jit(solution)/shard_map/ppermute | solution.py:17
  92.9 2.2 %collective-permute-done.3 = bf16[512,1,512]{0,2,1:T(8,128)(2,1)S(1)} collective-permute-done((bf16[512,1,512]{0,2,1:T(8,128)(2,1)S(1)}, bf16[512,1,512]{0,2,1:T(8,128)(2,1)S(1)}, u32[]{:S(2)}, u32[]{:S(2)}) %collective-permute-start.3) | collective-permute-done | bytes 524320 | tf_op jit(solution)/shard_map/ppermute | solution.py:18
  95.1 0.0 copy-done.3
  95.1 1.3 %fusion.3 = (f32[512]{0:T(512)S(1)}, f32[512]{0:T(512)S(1)}, f32[512,2,512]{0,2,1:T(8,128)S(1)}) fusion(bf16[1024,512]{1,0:T(8,128)(2,1)S(1)} %get-tuple-element.25, f32[2,512]{1,0:T(2,128)S(1)} %copy-done.3, bf16[512,2,512]{0,2,1:T(8,128)(2,1)S(1)} %bitcast.23, f32[512,2,8,64]{0,3,2,1:T(8,128)S(1)} %fusion.8, ...), kind=kLoop, calls=%fused_computation.7 | loop fusion | flops 8911872 | bytes 7348224 | tf_op jit(solution)/shard_map/reduce_sum | solution.py:54
  96.4 20.7 %all-reduce = (f32[512]{0:T(512)S(1)}, f32[512]{0:T(512)S(1)}, f32[512]{0:T(512)S(1)}) all-reduce(f32[512]{0:T(512)S(1)} %get-tuple-element.7, f32[512]{0:T(512)S(1)} %get-tuple-element.24, f32[512]{0:T(512)S(1)} %get-tuple-element.6), channel_id=1, replica_groups=mesh['grid'=8,'band'=4] {'grid'}, use_global_device_ids=true, to_apply=%region_5.6 | all-reduce | flops 1536 | bytes 12288 | tf_op jit(solution)/shard_map/psum | solution.py:57
  117.1 1.4 %fusion.6 = bf16[512,2,512]{0,2,1:T(8,128)(2,1)} fusion(f32[512,2,512]{0,2,1:T(8,128)S(1)} %get-tuple-element.11, f32[512]{0:T(512)S(1)} %get-tuple-element.23, f32[512]{0:T(512)S(1)} %get-tuple-element.22, bf16[1024,512]{1,0:T(8,128)(2,1)S(1)} %get-tuple-element.25), kind=kLoop, calls=%fused_computation.10 | loop fusion | flops 2621440 | bytes 4198400 | tf_op jit(solution)/shard_map/convert_element_type | solution.py:64
  118.4 3.7 %copy.13 = bf16[512,2,512]{2,1,0:T(2,128)(2,1)} copy(bf16[512,2,512]{0,2,1:T(8,128)(2,1)} %fusion.6) | data formatting | bytes 2097152
  (2 shorter events, 0.1 us)
Async XLA Ops:
  0.6 15.2 %collective-permute-start = (bf16[512,2,512]{2,1,0:T(2,128)(2,1)}, bf16[512,2,512]{2,1,0:T(2,128)(2,1)S(1)}, u32[]{:S(2)}, u32[]{:S(2)}) collective-permute-start(bf16[512,2,512]{2,1,0:T(2,128)(2,1)} %param.3), channel_id=1, source_target_pairs={{0,1},{1,2},{2,3},{3,0},{4,5},{5,6},{6,7},{7,4},{8,9},{9,10},{10,1... | collective-permute-start | bytes 3145736 | tf_op jit(solution)/shard_map/ppermute | solution.py:44
  15.8 14.2 %collective-permute-start.1 = (bf16[512,2,512]{2,1,0:T(2,128)(2,1)S(1)}, bf16[512,2,512]{2,1,0:T(2,128)(2,1)S(1)}, u32[]{:S(2)}, u32[]{:S(2)}) collective-permute-start(bf16[512,2,512]{2,1,0:T(2,128)(2,1)S(1)} %collective-permute-done), channel_id=1, source_target_pairs={{0,1},{1,2},{2,3},{3,0},{4,5},{5,6},{6,7},{7,4},{8,9},{9,10},{10,1... | collective-permute-start | bytes 3145736 | tf_op jit(solution)/shard_map/ppermute | solution.py:44
  30.0 14.2 %collective-permute-start.2 = (bf16[512,2,512]{2,1,0:T(2,128)(2,1)S(1)}, bf16[512,2,512]{2,1,0:T(2,128)(2,1)S(1)}, u32[]{:S(2)}, u32[]{:S(2)}) collective-permute-start(bf16[512,2,512]{2,1,0:T(2,128)(2,1)S(1)} %collective-permute-done.1), channel_id=1, source_target_pairs={{0,1},{1,2},{2,3},{3,0},{4,5},{5,6},{6,7},{7,4},{8,9},{9,10},{10,1... | collective-permute-start | bytes 3145736 | tf_op jit(solution)/shard_map/ppermute | solution.py:44
  45.0 1.6 %copy-start.1 = (bf16[512,2,512]{2,1,0:T(2,128)(2,1)S(1)}, bf16[512,2,512]{2,1,0:T(2,128)(2,1)}, u32[]{:S(2)}) copy-start(bf16[512,2,512]{2,1,0:T(2,128)(2,1)} %param.3) | copy-start | bytes 3145732
  53.7 2.2 %copy-start.4 = (f32[512,2048]{1,0:T(8,128)S(1)}, f32[512,2048]{1,0:T(8,128)}, u32[]{:S(2)}) copy-start(f32[512,2048]{1,0:T(8,128)} %param.4) | copy-start | bytes 12582916
  68.8 24.1 %collective-permute-start.4 = (bf16[512,1,512]{0,2,1:T(8,128)(2,1)S(1)}, bf16[512,1,512]{0,2,1:T(8,128)(2,1)S(1)}, u32[]{:S(2)}, u32[]{:S(2)}) collective-permute-start(bf16[512,1,512]{0,2,1:T(8,128)(2,1)S(1)} %get-tuple-element.13), channel_id=1, source_target_pairs={{0,4},{4,8},{8,12},{12,16},{16,20},{20,24},{24,28},{28,0},{1,5},{5... | collective-permute-start | bytes 1572872 | tf_op jit(solution)/shard_map/ppermute | solution.py:17
  71.2 3.6 %copy-start = (f32[512,2,8,63]{0,3,2,1:T(8,128)S(1)}, f32[512,2,8,63]{0,3,2,1:T(8,128)}, u32[]{:S(2)}) copy-start(f32[512,2,8,63]{0,3,2,1:T(8,128)} %get-tuple-element.15) | copy-start | bytes 6193156
  71.2 3.6 %copy-start.2 = (f32[512,2,1,64]{0,3,2,1:T(8,128)S(1)}, f32[512,2,1,64]{0,3,2,1:T(8,128)}, u32[]{:S(2)}) copy-start(f32[512,2,1,64]{0,3,2,1:T(8,128)} %get-tuple-element.21) | copy-start | bytes 786436
  71.2 23.9 %collective-permute-start.3 = (bf16[512,1,512]{0,2,1:T(8,128)(2,1)S(1)}, bf16[512,1,512]{0,2,1:T(8,128)(2,1)S(1)}, u32[]{:S(2)}, u32[]{:S(2)}) collective-permute-start(bf16[512,1,512]{0,2,1:T(8,128)(2,1)S(1)} %get-tuple-element.12), channel_id=1, source_target_pairs={{4,0},{8,4},{12,8},{16,12},{20,16},{24,20},{28,24},{0,28},{5,1},{9... | collective-permute-start | bytes 1572872 | tf_op jit(solution)/shard_map/ppermute | solution.py:18
  74.8 20.3 %copy-start.3 = (f32[2,512]{1,0:T(2,128)S(1)}, f32[2,512]{1,0:T(2,128)}, u32[]{:S(2)}) copy-start(f32[2,512]{1,0:T(2,128)} %param.5) | copy-start | bytes 12292
